TPU v7x, 64 devices: a 2x2x8 block of a 4x4x8 slice. The times are simulated.
64 devices in a mesh: data: 4 (over x, y), expert: 16 (over z, core).
Axes of the slice: x: 2, y: 2, z: 8, core: 2. Of those that a mesh axis runs over, the one named last changes fastest.
The devices are a block of a 4x4x8 slice.
Arguments:
- x_tok: bfloat16 [4096, 2048], P(('data', 'expert')), parts along dimension 0
- topk_idx: int32 [4096, 6], P(('data', 'expert')), parts along dimension 0
- topk_w: float32 [4096, 6], P(('data', 'expert')), parts along dimension 0
- w_up: bfloat16 [64, 2048, 1408], P('expert')
- w_down: bfloat16 [64, 1408, 2048], P('expert')
Outputs:
- output: bfloat16 [4096, 2048], P(('data', 'expert')), parts along dimension 0
There are 4 independent parts. A program takes and returns all parts, laid end to end along the dimension named above; an argument that names none is the same for every part.
All inputs are finite; a program needn't handle non-finite values.
Results may differ from a plain program's by a relative error of at most 0.0013.
Values are sent between devices in bfloat16 or wider.
A program may use at most 768 MiB of HBM per device.

v0:
```python
import jax
import jax.numpy as jnp
from jax import lax
from jax.sharding import PartitionSpec as P, NamedSharding


def route_slots(idx_loc, n_exp, slot_cap):
    top_k = idx_loc.shape[1]
    pair_exp = idx_loc.reshape(-1)
    n_pairs = pair_exp.shape[0]
    sort_order = jnp.argsort(pair_exp, stable=True)
    pair_rank = jnp.argsort(sort_order, stable=True)
    counts = jnp.bincount(pair_exp, length=n_exp)
    starts = jnp.cumsum(counts) - counts
    slot_src = jnp.minimum(starts[:, None] + jnp.arange(slot_cap)[None, :], n_pairs - 1)
    slot_tok = (sort_order[slot_src] // top_k).reshape(-1)
    pair_slot = pair_exp * slot_cap + pair_rank - starts[pair_exp]
    return slot_tok, pair_slot


def solution(mesh):
    group_size = mesh.shape['expert']

    def local_moe(x_loc, idx_loc, gate_loc, up_loc, down_loc):
        tok_dev, d_model = x_loc.shape
        top_k = idx_loc.shape[1]
        exp_local = up_loc.shape[0]
        n_exp = exp_local * group_size
        slot_cap = min(4, n_exp // top_k) * tok_dev * top_k // n_exp
        slot_tok, pair_slot = route_slots(idx_loc, n_exp, slot_cap)
        send_rows = jnp.take(x_loc, slot_tok, axis=0).reshape(group_size, exp_local, slot_cap, d_model)
        recv_rows = lax.all_to_all(send_rows, 'expert', 0, 0, tiled=True)
        hidden = jnp.einsum('secm,emf->secf', recv_rows, up_loc, preferred_element_type=jnp.float32)
        hidden = jax.nn.gelu(hidden, approximate=True).astype(jnp.bfloat16)
        expert_out = jnp.einsum('secf,efm->secm', hidden, down_loc, preferred_element_type=jnp.float32).astype(jnp.bfloat16)
        back_rows = lax.all_to_all(expert_out, 'expert', 0, 0, tiled=True).reshape(n_exp * slot_cap, d_model)
        pair_out = jnp.take(back_rows, pair_slot, axis=0).reshape(tok_dev, top_k, d_model)
        combined = jnp.sum(gate_loc[:, :, None] * pair_out.astype(jnp.float32), axis=1)
        return combined.astype(jnp.bfloat16)

    tok_spec = P(('data', 'expert'), None)
    w_spec = P('expert', None, None)
    return jax.shard_map(local_moe, mesh=mesh, in_specs=(tok_spec, tok_spec, tok_spec, w_spec, w_spec), out_specs=tok_spec, check_vma=False)
```

profile of v0, /device:TPU:21, one launch (start us, length us, event | category | flops | bytes accessed | tf_op | source)
XLA Modules:
  0.0 381.5 jit_solution(737305846890331888)
XLA Ops:
  0.0 0.0 copy-start
  0.0 0.8 copy.16
  0.8 0.1 reshape.216
  1.0 0.1 reshape.215
  1.1 3.9 %scatter_custom_fusion = s32[64]{0:T(128)S(1)} fusion(s32[384]{0:T(512)S(1)} %maximum_reduce_fusion, s32[384]{0:T(512)S(1)} %broadcast.315, s32[]{:T(128)} %constant.23.clone.1), kind=kCustom, calls=%fused_computation.104 | custom fusion | flops 384 | bytes 260 | tf_op jit(solution)/shard_map/scatter-add | solution.py:13
  5.0 0.1 copy.18
  5.1 0.1 reduce-window.9
  5.2 0.1 reduce.2
  5.3 0.1 compare_select_fusion.1
  5.4 0.1 reshape.293
  5.5 3.8 sort.31
  9.3 9.5 %gather_fusion = s32[1536]{0:T(1024)S(1)} fusion(s32[384]{0:T(512)S(1)} %get-tuple-element.7, s32[2048]{0:T(1024)S(1)} %pad_clamp_fusion.1), kind=kCustom, calls=%fused_computation | custom fusion | bytes 18432 | tf_op jit(solution)/shard_map/gather | solution.py:16
  18.8 0.1 div.24
  18.9 0.1 and.36
  19.1 0.0 copy-done
  19.1 7.1 %gather_fusion.1 = bf16[1536,2048]{1,0:T(8,128)(2,1)} fusion(bf16[64,2048]{1,0:T(8,128)(2,1)S(1)} %copy-done, s32[2048]{0:T(1024)S(1)} %pad_clamp_fusion), kind=kCustom, calls=%fused_computation.1 | custom fusion | bytes 12589056 | tf_op jit(solution)/shard_map/jit(_take)/gather | solution.py:31
  26.2 3.4 broadcast_select_fusion
  29.6 151.5 %all_to_all.10 = bf16[16,4,24,2048]{3,2,1,0:T(8,128)(2,1)} all-to-all(bf16[16,4,24,2048]{3,2,1,0:T(8,128)(2,1)S(1)} %broadcast_select_fusion), channel_id=1, replica_groups=mesh['data'=4,'expert'=16] {'expert'}, dimensions={0} | all-to-all | bytes 12582912 | tf_op jit(solution)/shard_map/all_to_all | solution.py:32
  181.1 20.7 %fusion.11 = bf16[16,4,24,1408]{3,2,0,1:T(8,128)(2,1)} fusion(bf16[4,2048,1408]{2,1,0:T(8,128)(2,1)} %param.8, bf16[16,4,24,2048]{3,2,1,0:T(8,128)(2,1)} %all_to_all.10), kind=kOutput, calls=%fused_computation.16 | convolution fusion | flops 8877834240 | bytes 33685504 | tf_op jit(solution)/shard_map/secm,emf->secf/dot_general | solution.py:33
  201.8 15.7 %convert_bitcast_fusion = bf16[16,4,24,2048]{3,2,0,1:T(8,128)(2,1)S(1)} fusion(bf16[16,4,24,1408]{3,2,0,1:T(8,128)(2,1)} %fusion.11, bf16[4,1408,2048]{2,1,0:T(8,128)(2,1)} %param.9), kind=kOutput, calls=%fused_computation.18 | convolution fusion | flops 8861515776 | bytes 33685504 | tf_op jit(solution)/shard_map/secf,efm->secm/dot_general | solution.py:35
  217.5 3.5 copy.20
  221.0 0.0 copy-start.2
  221.0 5.1 %all-to-all-start.1 = ((bf16[16,4,24,2048]{3,2,1,0:T(8,128)(2,1)}), bf16[16,4,24,2048]{3,2,1,0:T(8,128)(2,1)}, u32[]{:S(2)}, u32[]{:S(2)}) async-start(bf16[16,4,24,2048]{3,2,1,0:T(8,128)(2,1)} %copy.20), calls=%async_computation.1 | async-start | bytes 12582912 | tf_op jit(solution)/shard_map/all_to_all | solution.py:36
  226.1 3.8 sort.32
  229.9 0.7 fusion.27
  230.6 0.7 fusion.24
  231.3 0.7 fusion.25
  232.0 0.7 fusion.26
  232.8 4.5 %fusion.21 = (s32[384]{0:T(512)S(1)}, s32[384,1]{0,1:T(1,128)S(1)}) fusion(s32[]{:T(128)} %bitcast.58, s32[]{:T(128)} %bitcast.59, s32[]{:T(128)} %bitcast.60, s32[]{:T(128)} %bitcast.61, s32[]{:T(128)} %bitcast.62, s32[]{:T(128)} %bitcast.64, s32[]{:T(128)} %bitcast.63, s32[384,1]{0,1:T(1,128)S(1)} %reshape.216), kind=kLoop, calls=%fused_computation.102 | loop fusion | flops 5760 | bytes 4636 | tf_op jit(solution)/shard_map/gather | solution.py:17
  237.3 0.3 compare_reduce_fusion.56
  237.6 35.3 %compare_and_fusion.1 = (pred[384]{0:T(512)(128)(4,1)S(1)}, s32[384]{0:T(512)S(1)}) fusion(pred[384]{0:T(512)(128)(4,1)S(1)} %get-tuple-element.65, pred[384]{0:T(512)(128)(4,1)S(1)} %get-tuple-element.64, pred[384]{0:T(512)(128)(4,1)S(1)} %get-tuple-element.63, pred[384]{0:T(512)(128)(4,1)S(1)} %get-tuple-element.62, ...), kind=kLoop, calls=%fused_computation.101 | loop fusion | flops 25344 | bytes 28644 | tf_op jit(solution)/shard_map/jit(_take)/and | solution.py:37
  272.9 0.1 broadcast_in_dim.38
  273.0 0.0 copy-done.2
  273.0 0.1 copy.15
  273.1 93.8 %all-to-all-done.1 = bf16[16,4,24,2048]{3,2,1,0:T(8,128)(2,1)} async-done(((bf16[16,4,24,2048]{3,2,1,0:T(8,128)(2,1)}), bf16[16,4,24,2048]{3,2,1,0:T(8,128)(2,1)}, u32[]{:S(2)}, u32[]{:S(2)}) %all-to-all-start.1) | async-done | bytes 6291488 | tf_op jit(solution)/shard_map/all_to_all | solution.py:36
  367.0 0.0 copy-start.1
  367.0 8.7 %gather_fusion.2 = bf16[384,2048]{1,0:T(8,128)(2,1)} fusion(bf16[1536,2048]{1,0:T(8,128)(2,1)} %bitcast.72, s32[1024]{0:T(1024)S(1)} %pad_clamp_fusion.2), kind=kCustom, calls=%fused_computation.2 | custom fusion | bytes 3147264 | tf_op jit(solution)/shard_map/jit(_take)/gather | solution.py:37
  375.7 2.5 gather.23
  378.2 3.4 multiply_reduce_fusion
  381.5 0.0 copy-done.1
  (12 shorter events, 0.1 us)
Async XLA Ops:
  0.0 19.1 %copy-start = (bf16[64,2048]{1,0:T(8,128)(2,1)S(1)}, bf16[64,2048]{1,0:T(8,128)(2,1)}, u32[]{:S(2)}) copy-start(bf16[64,2048]{1,0:T(8,128)(2,1)} %param.5) | copy-start | bytes 786436
  221.0 52.0 %copy-start.2 = (f32[64,6]{0,1:T(8,128)S(1)}, f32[64,6]{0,1:T(8,128)}, u32[]{:S(2)}) copy-start(f32[64,6]{0,1:T(8,128)} %param.7) | copy-start | bytes 4612
  221.0 146.0 %all-to-all-start.1 = ((bf16[16,4,24,2048]{3,2,1,0:T(8,128)(2,1)}), bf16[16,4,24,2048]{3,2,1,0:T(8,128)(2,1)}, u32[]{:S(2)}, u32[]{:S(2)}) async-start(bf16[16,4,24,2048]{3,2,1,0:T(8,128)(2,1)} %copy.20), calls=%async_computation.1 | async-start | bytes 12582912 | tf_op jit(solution)/shard_map/all_to_all | solution.py:36
  367.0 14.5 %copy-start.1 = (bf16[64,2048]{1,0:T(8,128)(2,1)S(1)}, bf16[64,2048]{1,0:T(8,128)(2,1)}, u32[]{:S(2)}) copy-start(bf16[64,2048]{1,0:T(8,128)(2,1)} %param.5) | copy-start | bytes 786436
where the time goes:
time: 382 us
  blocking collectives  151 us (40%)
  waiting for transfers between devices  93.8 us (25%)
  other arithmetic  58.7 us (15%)
  matrix products  36.4 us (10%)
  local copies, waits for them, and re-layouts  35.8 us (9%)
  starting transfers between devices  5.1 us (1%)
    all_to_all x1, blocking collectives, local_moe(): recv_rows = lax.all_to_all(send_rows, 'expert', 0, 0, tiled=True)  151 us
    all_to_all x1, waiting for transfers between devices, local_moe(): lax.all_to_all(expert_out, 'expert', 0, 0, tiled=True)  93.8 us
    and x1, other arithmetic, local_moe(): jnp.take(back_rows, pair_slot, axis=0).reshape(tok_dev, top_k, d_model)  35.3 us
    dot_general x1, matrix products, local_moe(): jnp.einsum('secm,emf->secf', recv_rows, up_loc, preferred_element_type=jn...  20.7 us
    dot_general x1, matrix products, local_moe(): jnp.einsum('secf,efm->secm', hidden, down_loc, preferred_element_type=jnp...  15.7 us
    gather x2, local copies, waits for them, and re-layouts, local_moe(): jnp.take(back_rows, pair_slot, axis=0).reshape(tok_dev, top_k, d_model)  11.2 us
    gather x1, local copies, waits for them, and re-layouts, route_slots(): slot_tok = (sort_order[slot_src] // top_k).reshape(-1)  9.47 us
  transfers between devices with their start and end apart: 1, of which 1 were waited for; matrix products, arithmetic and copies ran while one was open for 12% of the time, Pallas kernels for 0%

commit v1 on v0

v1 whole, which is shorter than its diff:
```python
import functools

import jax
import jax.numpy as jnp
from jax import lax
from jax.experimental import pallas as pl
from jax.experimental.pallas import tpu as pltpu
from jax.sharding import PartitionSpec as P

MESH = pl.DeviceIdType.MESH
COLS = 256
LANES = 128
WD_SLOTS = 3


def moe_kernel(group, cap, x_hbm, meta_hbm, up_hbm, down_hbm, y_ref,
               wup, wd, xb, metab, xg, hid, cmat, ob, acc, psend, precv, rhalf, rfull,
               loc_sem, up_sem, wd_sem, ag_s, ag_r, mt_s, mt_r, pd_s, pd_r, pm_s, pm_r,
               ps_s, ps_r, h_s, h_r, f_s, f_r):
    n_chip = group // 2
    hops = n_chip // 2
    n_exp, d_model, d_ff = wup.shape
    tok = xb.shape[2]
    half = tok // 2
    chip_cap = 2 * cap
    slots = n_exp * chip_cap
    n_col = d_model // COLS
    f32, bf16 = jnp.float32, jnp.bfloat16

    me = lax.axis_index('expert')
    chip, core = me // 2, me % 2
    right = lax.rem(chip + 1, n_chip) * 2 + core
    left = lax.rem(chip + n_chip - 1, n_chip) * 2 + core
    partner = chip * 2 + 1 - core

    def remote(src, dst, send_sem, recv_sem, dev):
        return pltpu.make_async_remote_copy(src_ref=src, dst_ref=dst, send_sem=send_sem, recv_sem=recv_sem,
                                            device_id={'expert': dev}, device_id_type=MESH)

    x_copy = pltpu.make_async_copy(x_hbm, xb.at[0, 0], loc_sem.at[0])
    m_copy = pltpu.make_async_copy(meta_hbm, metab.at[0, 0], loc_sem.at[1])
    x_copy.start()
    m_copy.start()

    def up_copy(e):
        return pltpu.make_async_copy(up_hbm.at[e], wup.at[e], up_sem.at[e])

    def wd_copy(c):
        slot = lax.rem(c, WD_SLOTS)
        cols = pl.ds(pl.multiple_of(c * COLS, COLS), COLS)
        return pltpu.make_async_copy(down_hbm.at[:, :, cols], wd.at[slot], wd_sem.at[slot])

    for e in range(n_exp):
        up_copy(e).start()
    for c in range(min(WD_SLOTS, n_col)):
        wd_copy(jnp.int32(c)).start()

    barrier = pltpu.get_barrier_semaphore()
    for dev in (right, left, partner):
        pl.semaphore_signal(barrier, inc=1, device_id={'expert': dev}, device_id_type=MESH)
    pl.semaphore_wait(barrier, 3)
    x_copy.wait()
    m_copy.wait()

    steps = [[], []]
    for h in range(hops):
        for b in range(2):
            for way in range(2):
                if h < hops - 1 or b == way:
                    steps[way].append((h, b))
    n_step = len(steps[0])

    def slot_of(way, h):
        return h if way == 0 else (n_chip - h) % n_chip

    def ring_x(way, j):
        h, b = steps[way][j]
        rows = pl.ds(b * half, half)
        return remote(xb.at[slot_of(way, h), 0, rows], xb.at[slot_of(way, h + 1), 0, rows],
                      ag_s.at[way, j], ag_r.at[way, j], left if way else right)

    def ring_meta(way, h):
        return remote(metab.at[slot_of(way, h), 0], metab.at[slot_of(way, h + 1), 0],
                      mt_s.at[way, h], mt_r.at[way, h], left if way else right)

    def pair_x(o, b):
        rows = pl.ds(b * half, half)
        return remote(xb.at[o, 0, rows], xb.at[o, 1, rows], pd_s.at[o, b], pd_r.at[o, b], partner)

    def pair_meta(o):
        return remote(metab.at[o, 0], metab.at[o, 1], pm_s.at[o], pm_r.at[o], partner)

    meta_hops = (hops, hops - 1)

    tri_r = lax.broadcasted_iota(jnp.int32, (LANES, LANES), 0)
    tri_c = lax.broadcasted_iota(jnp.int32, (LANES, LANES), 1)
    before = jnp.logical_and(tri_r < tri_c, (tri_r >= tok) == (tri_c >= tok))
    tri = jnp.where(before, 1.0, 0.0).astype(bf16)
    lane8 = lax.broadcasted_iota(jnp.int32, (8, LANES), 1)
    row8 = lax.broadcasted_iota(jnp.int32, (8, LANES), 0)
    slot_row = lax.broadcasted_iota(jnp.int32, (chip_cap, LANES), 0).astype(f32)

    def route(o):
        m0, m1 = metab[o, 0], metab[o, 1]
        low = lane8 < tok
        ids = jnp.where(low, m0, pltpu.roll(m1, tok, 1))
        gates = jnp.where(low, pltpu.roll(m0, tok, 1), m1)
        mask = jnp.zeros((8, LANES), f32)
        gate_rows = []
        for e in range(n_exp):
            hit = ids == (me * n_exp + e).astype(f32)
            row = jnp.sum(jnp.where(hit, 1.0, 0.0), axis=0, keepdims=True)
            mask = jnp.where(row8 == e, row, mask)
            gate_rows.append(jnp.sum(jnp.where(hit, gates, 0.0), axis=0, keepdims=True))
        pos = jnp.dot(mask.astype(bf16), tri, preferred_element_type=f32)
        pos = jnp.where(mask > 0.5, pos + jnp.where(low, 0.0, float(cap)), -1.0)
        pick = [jnp.where(slot_row == pos[e:e + 1, :], 1.0, 0.0) for e in range(n_exp)]
        pick_all = jnp.concatenate(pick, axis=0).astype(bf16)
        for n in range(d_model // COLS):
            cols = pl.ds(n * COLS, COLS)
            rows_x = jnp.concatenate([xb[o, 0, :, cols], xb[o, 1, :, cols]], axis=0)
            got = jnp.dot(pick_all, rows_x, preferred_element_type=f32).astype(bf16)
            for e in range(n_exp):
                xg[e, pl.ds(o * chip_cap, chip_cap), cols] = got[e * chip_cap:(e + 1) * chip_cap]
        weighted = [pick[e] * gate_rows[e] for e in range(n_exp)]
        weighted.append(jnp.zeros((COLS - slots, LANES), f32))
        rest = jnp.transpose(jnp.concatenate(weighted, axis=0))
        for part in range(3):
            piece = rest.astype(bf16)
            cmat[o, pl.ds(part * LANES, LANES), :] = piece
            rest = rest - piece.astype(f32)

    for way in range(2):
        ring_meta(way, 0).start()
    for j in range(2):
        for way in range(2):
            ring_x(way, j).start()
    pair_meta(0).start()
    for b in range(2):
        pair_x(0, b).start()

    def routed(o):
        pair_meta(o).wait_recv()
        for b in range(2):
            pair_x(o, b).wait_recv()
        route(o)

    for j in range(n_step):
        h = steps[0][j][0]
        if steps[0][j][1] == 0:
            for way in range(2):
                if h < meta_hops[way]:
                    ring_meta(way, h).wait_recv()
                    if h + 1 < meta_hops[way]:
                        ring_meta(way, h + 1).start()
                    pair_meta(slot_of(way, h + 1)).start()
        for way in range(2):
            ring_x(way, j).wait_recv()
            nxt = (steps[way][j][0] + 1, steps[way][j][1])
            if nxt in steps[way]:
                ring_x(way, steps[way].index(nxt)).start()
            pair_x(slot_of(way, h + 1), steps[way][j][1]).start()
        if j == 0:
            routed(0)
        elif j % 2 == 0 and h >= 1:
            routed(slot_of(0, h))
            routed(slot_of(1, h))
    routed(hops)

    def up_expert(e, carry):
        up_copy(e).wait()

        def up_cols(start, width):
            cols = pl.ds(start, width)
            raw = jnp.dot(xg[e], wup[e, :, cols], preferred_element_type=f32)
            hid[e, :, cols] = jax.nn.gelu(raw, approximate=True).astype(bf16)

        def up_step(n, inner):
            up_cols(pl.multiple_of(n * COLS, COLS), COLS)
            return inner

        lax.fori_loop(0, d_ff // COLS, up_step, 0)
        if d_ff % COLS:
            up_cols(d_ff - d_ff % COLS, d_ff % COLS)
        return carry

    lax.fori_loop(0, n_exp, up_expert, 0)

    for o in range(n_chip):
        ob[o, pl.ds(slots, COLS - slots), :] = jnp.zeros((COLS - slots, COLS), bf16)

    def pair_sum(c):
        slot = lax.rem(c, 2)
        return remote(psend.at[slot], precv.at[c], ps_s.at[c], ps_r.at[c], partner)

    def half_sum(way, c):
        rows = pl.ds(way * half, half)
        return remote(acc.at[c, hops, rows], rhalf.at[way, c], h_s.at[way, c], h_r.at[way, c], left if way else right)

    def full_sum(way, k, c):
        o = hops + k if way == 0 else hops - k
        return remote(acc.at[c, o], rfull.at[way, k - 1, c], f_s.at[way, k - 1, c], f_r.at[way, k - 1, c],
                      left if way else right)

    def down_chunk(c):
        slot = lax.rem(c, WD_SLOTS)
        wd_copy(c).wait()
        for e in range(n_exp):
            out = jnp.dot(hid[e], wd[slot, e], preferred_element_type=f32).astype(bf16)
            for o in range(n_chip):
                ob[o, pl.ds(e * chip_cap, chip_cap), :] = out[o * chip_cap:(o + 1) * chip_cap]

        @pl.when(c + WD_SLOTS < n_col)
        def _():
            wd_copy(c + WD_SLOTS).start()

        @pl.when(c >= 2)
        def _():
            pair_sum(c - 2).wait_send()

        for o in range(n_chip):
            got = jnp.dot(cmat[o], ob[o], preferred_element_type=f32)
            total = got[:LANES] + got[LANES:2 * LANES] + got[2 * LANES:]
            acc[c, o] = total[:tok]
            psend[lax.rem(c, 2), o] = total[tok:]
        pair_sum(c).start()

    def step(i, carry):
        @pl.when(i < n_col)
        def _():
            down_chunk(i)

        for k in range(1, hops + 1):
            c = i - k

            @pl.when(jnp.logical_and(c >= 0, c < n_col))
            def _():
                if k == 1:
                    for way in range(2):
                        half_sum(way, c).wait_recv()
                        o = hops + 1 if way == 0 else hops - 1
                        rows = pl.ds(way * half, half)
                        acc[c, o, rows, :] = acc[c, o, rows, :] + rhalf[way, c]
                        full_sum(way, 1, c).start()
                elif k < hops:
                    for way in range(2):
                        full_sum(way, k - 1, c).wait_recv()
                        o = hops + k if way == 0 else hops - k
                        acc[c, o] = acc[c, o] + rfull[way, k - 2, c]
                        full_sum(way, k, c).start()
                else:
                    total = acc[c, 0]
                    for way in range(2):
                        full_sum(way, hops - 1, c).wait_recv()
                        total = total + rfull[way, hops - 2, c]
                    cols = pl.ds(pl.multiple_of(c * COLS, COLS), COLS)
                    y_ref[:, cols] = total.astype(bf16)

        @pl.when(i < n_col)
        def _():
            pair_sum(i).wait_recv()
            for o in range(n_chip):
                acc[i, o] = acc[i, o] + precv[i, o]
            for way in range(2):
                half_sum(way, i).start()
        return carry

    lax.fori_loop(0, n_col + hops, step, 0)

    for way in range(2):
        for j in range(n_step):
            ring_x(way, j).wait_send()
        for h in range(meta_hops[way]):
            ring_meta(way, h).wait_send()
    for o in range(n_chip):
        pair_meta(o).wait_send()
        for b in range(2):
            pair_x(o, b).wait_send()

    def drain(c, carry):
        for way in range(2):
            half_sum(way, c).wait_send()
            for k in range(1, hops):
                full_sum(way, k, c).wait_send()

        @pl.when(c >= n_col - 2)
        def _():
            pair_sum(c).wait_send()
        return carry

    lax.fori_loop(0, n_col, drain, 0)


def solution(mesh):
    group = mesh.shape['expert']
    n_chip = group // 2
    hops = n_chip // 2

    def local_moe(x_loc, idx_loc, gate_loc, up_loc, down_loc):
        tok, d_model = x_loc.shape
        top_k = idx_loc.shape[1]
        n_exp, _, d_ff = up_loc.shape
        total_exp = n_exp * group
        cap = min(4, total_exp // top_k) * tok * top_k // total_exp
        n_col = d_model // COLS
        bf16, f32 = jnp.bfloat16, jnp.float32
        ids = jnp.pad(idx_loc.T.astype(f32), ((0, 8 - top_k), (0, 0)), constant_values=-1.0)
        gates = jnp.pad(gate_loc.T, ((0, 8 - top_k), (0, 0)))
        meta = jnp.concatenate([ids, gates], axis=1)
        dma = pltpu.SemaphoreType.DMA
        any_spec = pl.BlockSpec(memory_space=pl.ANY)
        n_step = 2 * hops - 1
        return pl.pallas_call(
            functools.partial(moe_kernel, group, cap),
            out_shape=jax.ShapeDtypeStruct((tok, d_model), bf16),
            in_specs=[any_spec] * 4,
            out_specs=pl.BlockSpec(memory_space=pltpu.VMEM),
            scratch_shapes=[
                pltpu.VMEM((n_exp, d_model, d_ff), bf16),
                pltpu.VMEM((WD_SLOTS, n_exp, d_ff, COLS), bf16),
                pltpu.VMEM((n_chip, 2, tok, d_model), bf16),
                pltpu.VMEM((n_chip, 2, 8, LANES), f32),
                pltpu.VMEM((n_exp, n_chip * 2 * cap, d_model), bf16),
                pltpu.VMEM((n_exp, n_chip * 2 * cap, d_ff), bf16),
                pltpu.VMEM((n_chip, 3 * LANES, COLS), bf16),
                pltpu.VMEM((n_chip, COLS, COLS), bf16),
                pltpu.VMEM((n_col, n_chip, tok, COLS), f32),
                pltpu.VMEM((2, n_chip, tok, COLS), f32),
                pltpu.VMEM((n_col, n_chip, tok, COLS), f32),
                pltpu.VMEM((2, n_col, tok // 2, COLS), f32),
                pltpu.VMEM((2, hops - 1, n_col, tok, COLS), f32),
                dma((2,)), dma((n_exp,)), dma((WD_SLOTS,)),
                dma((2, n_step)), dma((2, n_step)), dma((2, hops)), dma((2, hops)),
                dma((n_chip, 2)), dma((n_chip, 2)), dma((n_chip,)), dma((n_chip,)),
                dma((n_col,)), dma((n_col,)), dma((2, n_col)), dma((2, n_col)),
                dma((2, hops - 1, n_col)), dma((2, hops - 1, n_col)),
            ],
            compiler_params=pltpu.CompilerParams(
                collective_id=0, has_side_effects=True, vmem_limit_bytes=67043328),
        )(x_loc, meta, up_loc, down_loc)

    tok_spec = P(('data', 'expert'), None)
    w_spec = P('expert', None, None)
    return jax.shard_map(local_moe, mesh=mesh, in_specs=(tok_spec, tok_spec, tok_spec, w_spec, w_spec), out_specs=tok_spec, check_vma=False)
```

time: 382 us -> 122 us (0.32)
  the two profiles are of different devices: /device:TPU:21 before, /device:TPU:22 now
where the time goes in v1:
time: 122 us; the launch traced here: 121 us
  Pallas kernels  118 us (97%)
  other arithmetic  2.04 us (2%)
  local copies, waits for them, and re-layouts  1.67 us (1%)
    pallas_call x1, Pallas kernels, local_moe(): pl.pallas_call(functools.partial(moe_kernel, group, cap), out_shape=jax.S...  118 us

profile of v1, /device:TPU:22, one launch (start us, length us, event | category | flops | bytes accessed | tf_op | source)
XLA Modules:
  0.0 121.3 jit_solution(2180132301944920106)
XLA Ops:
  0.0 0.7 convert_bitcast_fusion
  0.7 1.4 %select_maximum_fusion.meta_hbm = f32[8,128]{1,0:T(8,128)} fusion(f32[6,64]{1,0:T(8,128)} %bitcast.3, f32[6,64]{1,0:T(8,128)S(1)} %convert_bitcast_fusion), kind=kLoop, calls=%fused_computation | loop fusion | flops 5120 | bytes 7168 | tf_op jit(solution)/shard_map/concatenate | solution.py:309
  2.0 117.6 %shard_map.55 = bf16[64,2048]{1,0:T(8,128)(2,1)} custom-call(bf16[64,2048]{1,0:T(8,128)(2,1)} %x_hbm.1, f32[8,128]{1,0:T(8,128)} %select_maximum_fusion.meta_hbm, bf16[4,2048,1408]{2,1,0:T(8,128)(2,1)} %up_hbm.1, bf16[4,1408,2048]{2,1,0:T(8,128)(2,1)} %down_hbm.1), custom_call_target="tpu_custom_call" | custom-call | tf_op jit(solution)/shard_map/pallas_call | solution.py:313
  119.7 1.7 %copy.7 = bf16[64,2048]{1,0:T(8,128)(2,1)} copy(bf16[64,2048]{1,0:T(8,128)(2,1)} %shard_map.55) | data formatting | bytes 524288

commit v2 on v1

--- a/solution.py
+++ b/solution.py
@@ -13,7 +13,7 @@
 WD_SLOTS = 3
 
 
-def moe_kernel(group, cap, x_hbm, meta_hbm, up_hbm, down_hbm, y_ref,
+def moe_kernel(group, cap, x_hbm, ids_ref, gate_ref, up_hbm, down_hbm, y_ref,
                wup, wd, xb, metab, xg, hid, cmat, ob, acc, psend, precv, rhalf, rfull,
                loc_sem, up_sem, wd_sem, ag_s, ag_r, mt_s, mt_r, pd_s, pd_r, pm_s, pm_r,
                ps_s, ps_r, h_s, h_r, f_s, f_r):
@@ -37,10 +37,12 @@
         return pltpu.make_async_remote_copy(src_ref=src, dst_ref=dst, send_sem=send_sem, recv_sem=recv_sem,
                                             device_id={'expert': dev}, device_id_type=MESH)
 
-    x_copy = pltpu.make_async_copy(x_hbm, xb.at[0, 0], loc_sem.at[0])
-    m_copy = pltpu.make_async_copy(meta_hbm, metab.at[0, 0], loc_sem.at[1])
+    x_copy = pltpu.make_async_copy(x_hbm, xb.at[0, 0], loc_sem)
     x_copy.start()
-    m_copy.start()
+    top_k = ids_ref.shape[0]
+    metab[0, 0] = jnp.full(metab.shape[2:], -1.0, f32)
+    metab[0, 0, pl.ds(0, top_k), pl.ds(0, tok)] = ids_ref[...].astype(f32)
+    metab[0, 0, pl.ds(8, top_k), pl.ds(0, tok)] = gate_ref[...]
 
     def up_copy(e):
         return pltpu.make_async_copy(up_hbm.at[e], wup.at[e], up_sem.at[e])
@@ -60,7 +62,6 @@
         pl.semaphore_signal(barrier, inc=1, device_id={'expert': dev}, device_id_type=MESH)
     pl.semaphore_wait(barrier, 3)
     x_copy.wait()
-    m_copy.wait()
 
     steps = [[], []]
     for h in range(hops):
@@ -92,6 +93,13 @@
 
     meta_hops = (hops, hops - 1)
 
+    order = [0]
+    for h in range(1, hops):
+        order += [h, n_chip - h]
+    order.append(hops)
+    place = {o: p for p, o in enumerate(order)}
+    bounds = [0, 3, 5, n_chip]
+
     tri_r = lax.broadcasted_iota(jnp.int32, (LANES, LANES), 0)
     tri_c = lax.broadcasted_iota(jnp.int32, (LANES, LANES), 1)
     before = jnp.logical_and(tri_r < tri_c, (tri_r >= tok) == (tri_c >= tok))
@@ -103,8 +111,8 @@
     def route(o):
         m0, m1 = metab[o, 0], metab[o, 1]
         low = lane8 < tok
-        ids = jnp.where(low, m0, pltpu.roll(m1, tok, 1))
-        gates = jnp.where(low, pltpu.roll(m0, tok, 1), m1)
+        ids = jnp.where(low, m0[:8], pltpu.roll(m1[:8], tok, 1))
+        gates = jnp.where(low, m0[8:], pltpu.roll(m1[8:], tok, 1))
         mask = jnp.zeros((8, LANES), f32)
         gate_rows = []
         for e in range(n_exp):
@@ -121,7 +129,7 @@
             rows_x = jnp.concatenate([xb[o, 0, :, cols], xb[o, 1, :, cols]], axis=0)
             got = jnp.dot(pick_all, rows_x, preferred_element_type=f32).astype(bf16)
             for e in range(n_exp):
-                xg[e, pl.ds(o * chip_cap, chip_cap), cols] = got[e * chip_cap:(e + 1) * chip_cap]
+                xg[e, pl.ds(place[o] * chip_cap, chip_cap), cols] = got[e * chip_cap:(e + 1) * chip_cap]
         weighted = [pick[e] * gate_rows[e] for e in range(n_exp)]
         weighted.append(jnp.zeros((COLS - slots, LANES), f32))
         rest = jnp.transpose(jnp.concatenate(weighted, axis=0))
@@ -145,7 +153,7 @@
             pair_x(o, b).wait_recv()
         route(o)
 
-    for j in range(n_step):
+    def gather_step(j):
         h = steps[0][j][0]
         if steps[0][j][1] == 0:
             for way in range(2):
@@ -160,38 +168,52 @@
             if nxt in steps[way]:
                 ring_x(way, steps[way].index(nxt)).start()
             pair_x(slot_of(way, h + 1), steps[way][j][1]).start()
-        if j == 0:
-            routed(0)
-        elif j % 2 == 0 and h >= 1:
-            routed(slot_of(0, h))
-            routed(slot_of(1, h))
+
+    def up_rows(phase, first, last):
+        rows = pl.ds(bounds[phase] * chip_cap, (bounds[phase + 1] - bounds[phase]) * chip_cap)
+
+        def expert(e, carry):
+            if phase == 0:
+                up_copy(e).wait()
+            for start in range(0, d_ff, COLS):
+                cols = pl.ds(start, min(COLS, d_ff - start))
+                raw = jnp.dot(xg[e, rows, :], wup[e, :, cols], preferred_element_type=f32)
+                hid[e, rows, cols] = jax.nn.gelu(raw, approximate=True).astype(bf16)
+            return carry
+
+        lax.fori_loop(first, last, expert, 0)
+
+    routed(0)
+    gather_step(0)
+    gather_step(1)
+    routed(1)
+    routed(n_chip - 1)
+    gather_step(2)
+    up_rows(0, 0, n_exp // 2)
+    gather_step(3)
+    up_rows(0, n_exp // 2, n_exp)
+    gather_step(4)
+    routed(2)
+    routed(n_chip - 2)
+    up_rows(1, 0, 1)
+    gather_step(5)
+    up_rows(1, 1, n_exp - 1)
+    gather_step(6)
+    up_rows(1, n_exp - 1, n_exp)
+    routed(3)
+    routed(n_chip - 3)
     routed(hops)
-
-    def up_expert(e, carry):
-        up_copy(e).wait()
-
-        def up_cols(start, width):
-            cols = pl.ds(start, width)
-            raw = jnp.dot(xg[e], wup[e, :, cols], preferred_element_type=f32)
-            hid[e, :, cols] = jax.nn.gelu(raw, approximate=True).astype(bf16)
-
-        def up_step(n, inner):
-            up_cols(pl.multiple_of(n * COLS, COLS), COLS)
-            return inner
-
-        lax.fori_loop(0, d_ff // COLS, up_step, 0)
-        if d_ff % COLS:
-            up_cols(d_ff - d_ff % COLS, d_ff % COLS)
-        return carry
-
-    lax.fori_loop(0, n_exp, up_expert, 0)
+    up_rows(2, 0, n_exp)
 
     for o in range(n_chip):
         ob[o, pl.ds(slots, COLS - slots), :] = jnp.zeros((COLS - slots, COLS), bf16)
 
-    def pair_sum(c):
+    def pair_sum(c, k):
         slot = lax.rem(c, 2)
-        return remote(psend.at[slot], precv.at[c], ps_s.at[c], ps_r.at[c], partner)
+        part = pl.ds(k, 1 if k == 0 else n_chip - 1)
+        return remote(psend.at[slot, part], precv.at[c, part], ps_s.at[c, k], ps_r.at[c, k], partner)
+
+    far_first = order[::-1]
 
     def half_sum(way, c):
         rows = pl.ds(way * half, half)
@@ -208,7 +230,7 @@
         for e in range(n_exp):
             out = jnp.dot(hid[e], wd[slot, e], preferred_element_type=f32).astype(bf16)
             for o in range(n_chip):
-                ob[o, pl.ds(e * chip_cap, chip_cap), :] = out[o * chip_cap:(o + 1) * chip_cap]
+                ob[o, pl.ds(e * chip_cap, chip_cap), :] = out[place[o] * chip_cap:(place[o] + 1) * chip_cap]
 
         @pl.when(c + WD_SLOTS < n_col)
         def _():
@@ -216,14 +238,17 @@
 
         @pl.when(c >= 2)
         def _():
-            pair_sum(c - 2).wait_send()
-
-        for o in range(n_chip):
+            for k in range(2):
+                pair_sum(c - 2, k).wait_send()
+
+        for p, o in enumerate(far_first):
             got = jnp.dot(cmat[o], ob[o], preferred_element_type=f32)
             total = got[:LANES] + got[LANES:2 * LANES] + got[2 * LANES:]
             acc[c, o] = total[:tok]
-            psend[lax.rem(c, 2), o] = total[tok:]
-        pair_sum(c).start()
+            psend[lax.rem(c, 2), p] = total[tok:]
+            if p == 0:
+                pair_sum(c, 0).start()
+        pair_sum(c, 1).start()
 
     def step(i, carry):
         @pl.when(i < n_col)
@@ -258,11 +283,13 @@
 
         @pl.when(i < n_col)
         def _():
-            pair_sum(i).wait_recv()
-            for o in range(n_chip):
-                acc[i, o] = acc[i, o] + precv[i, o]
+            pair_sum(i, 0).wait_recv()
+            acc[i, hops] = acc[i, hops] + precv[i, 0]
             for way in range(2):
                 half_sum(way, i).start()
+            pair_sum(i, 1).wait_recv()
+            for p, o in enumerate(far_first[1:], 1):
+                acc[i, o] = acc[i, o] + precv[i, p]
         return carry
 
     lax.fori_loop(0, n_col + hops, step, 0)
@@ -285,7 +312,8 @@
 
         @pl.when(c >= n_col - 2)
         def _():
-            pair_sum(c).wait_send()
+            for k in range(2):
+                pair_sum(c, k).wait_send()
         return carry
 
     lax.fori_loop(0, n_col, drain, 0)
@@ -304,22 +332,20 @@
         cap = min(4, total_exp // top_k) * tok * top_k // total_exp
         n_col = d_model // COLS
         bf16, f32 = jnp.bfloat16, jnp.float32
-        ids = jnp.pad(idx_loc.T.astype(f32), ((0, 8 - top_k), (0, 0)), constant_values=-1.0)
-        gates = jnp.pad(gate_loc.T, ((0, 8 - top_k), (0, 0)))
-        meta = jnp.concatenate([ids, gates], axis=1)
         dma = pltpu.SemaphoreType.DMA
         any_spec = pl.BlockSpec(memory_space=pl.ANY)
+        vmem_spec = pl.BlockSpec(memory_space=pltpu.VMEM)
         n_step = 2 * hops - 1
         return pl.pallas_call(
             functools.partial(moe_kernel, group, cap),
             out_shape=jax.ShapeDtypeStruct((tok, d_model), bf16),
-            in_specs=[any_spec] * 4,
-            out_specs=pl.BlockSpec(memory_space=pltpu.VMEM),
+            in_specs=[any_spec, vmem_spec, vmem_spec, any_spec, any_spec],
+            out_specs=vmem_spec,
             scratch_shapes=[
                 pltpu.VMEM((n_exp, d_model, d_ff), bf16),
                 pltpu.VMEM((WD_SLOTS, n_exp, d_ff, COLS), bf16),
                 pltpu.VMEM((n_chip, 2, tok, d_model), bf16),
-                pltpu.VMEM((n_chip, 2, 8, LANES), f32),
+                pltpu.VMEM((n_chip, 2, 16, LANES), f32),
                 pltpu.VMEM((n_exp, n_chip * 2 * cap, d_model), bf16),
                 pltpu.VMEM((n_exp, n_chip * 2 * cap, d_ff), bf16),
                 pltpu.VMEM((n_chip, 3 * LANES, COLS), bf16),
@@ -329,15 +355,15 @@
                 pltpu.VMEM((n_col, n_chip, tok, COLS), f32),
                 pltpu.VMEM((2, n_col, tok // 2, COLS), f32),
                 pltpu.VMEM((2, hops - 1, n_col, tok, COLS), f32),
-                dma((2,)), dma((n_exp,)), dma((WD_SLOTS,)),
+                dma, dma((n_exp,)), dma((WD_SLOTS,)),
                 dma((2, n_step)), dma((2, n_step)), dma((2, hops)), dma((2, hops)),
                 dma((n_chip, 2)), dma((n_chip, 2)), dma((n_chip,)), dma((n_chip,)),
-                dma((n_col,)), dma((n_col,)), dma((2, n_col)), dma((2, n_col)),
+                dma((n_col, 2)), dma((n_col, 2)), dma((2, n_col)), dma((2, n_col)),
                 dma((2, hops - 1, n_col)), dma((2, hops - 1, n_col)),
             ],
             compiler_params=pltpu.CompilerParams(
                 collective_id=0, has_side_effects=True, vmem_limit_bytes=67043328),
-        )(x_loc, meta, up_loc, down_loc)
+        )(x_loc, idx_loc.T, gate_loc.T, up_loc, down_loc)
 
     tok_spec = P(('data', 'expert'), None)
     w_spec = P('expert', None, None)

time: 122 us -> 111 us (0.910)
  Pallas kernels: 118 us -> 109 us
  other arithmetic: 2.04 us -> 0 us
    pallas_call x1, Pallas kernels: 118 us -> 109 us  [local_moe(): pl.pallas_call(functools.partial(moe_kernel, group, cap), out_shape=jax.S...]
    concatenate x1 -> x0, other arithmetic: 1.35 us -> none  [local_moe(): meta = jnp.concatenate([ids, gates], axis=1)]
where the time goes in v2:
time: 111 us
  Pallas kernels  109 us (98%)
  local copies, waits for them, and re-layouts  1.67 us (2%)
    pallas_call x1, Pallas kernels, local_moe(): pl.pallas_call(functools.partial(moe_kernel, group, cap), out_shape=jax.S...  109 us

profile of v2, /device:TPU:22, one launch (start us, length us, event | category | flops | bytes accessed | tf_op | source)
XLA Modules:
  0.0 110.6 jit_solution(9098413242395423994)
XLA Ops:
  0.0 108.9 %shard_map.55 = bf16[64,2048]{1,0:T(8,128)(2,1)} custom-call(bf16[64,2048]{1,0:T(8,128)(2,1)} %x_hbm.1, s32[6,64]{1,0:T(8,128)} %bitcast.2, f32[6,64]{1,0:T(8,128)} %bitcast.3, bf16[4,2048,1408]{2,1,0:T(8,128)(2,1)} %up_hbm.1, bf16[4,1408,2048]{2,1,0:T(8,128)(2,1)} %down_hbm.1), custom_call_target="tpu_custom_call" | custom-call | tf_op jit(solution)/shard_map/pallas_call | solution.py:339
  109.0 1.7 %copy.7 = bf16[64,2048]{1,0:T(8,128)(2,1)} copy(bf16[64,2048]{1,0:T(8,128)(2,1)} %shard_map.55) | data formatting | bytes 524288

commit v3 on v2

--- a/solution.py
+++ b/solution.py
@@ -192,16 +192,15 @@
     up_rows(0, 0, n_exp // 2)
     gather_step(3)
     up_rows(0, n_exp // 2, n_exp)
-    gather_step(4)
     routed(2)
     routed(n_chip - 2)
-    up_rows(1, 0, 1)
+    gather_step(4)
+    up_rows(1, 0, n_exp // 2)
     gather_step(5)
-    up_rows(1, 1, n_exp - 1)
-    gather_step(6)
-    up_rows(1, n_exp - 1, n_exp)
+    up_rows(1, n_exp // 2, n_exp)
     routed(3)
     routed(n_chip - 3)
+    gather_step(6)
     routed(hops)
     up_rows(2, 0, n_exp)
 
@@ -254,9 +253,16 @@
         @pl.when(i < n_col)
         def _():
             down_chunk(i)
+            pair_sum(i, 0).wait_recv()
+            acc[i, hops] = acc[i, hops] + precv[i, 0]
+            for way in range(2):
+                half_sum(way, i).start()
+            pair_sum(i, 1).wait_recv()
+            for p, o in enumerate(far_first[1:], 1):
+                acc[i, o] = acc[i, o] + precv[i, p]
 
         for k in range(1, hops + 1):
-            c = i - k
+            c = i - k if k < hops else i - hops - 1
 
             @pl.when(jnp.logical_and(c >= 0, c < n_col))
             def _():
@@ -281,18 +287,9 @@
                     cols = pl.ds(pl.multiple_of(c * COLS, COLS), COLS)
                     y_ref[:, cols] = total.astype(bf16)
 
-        @pl.when(i < n_col)
-        def _():
-            pair_sum(i, 0).wait_recv()
-            acc[i, hops] = acc[i, hops] + precv[i, 0]
-            for way in range(2):
-                half_sum(way, i).start()
-            pair_sum(i, 1).wait_recv()
-            for p, o in enumerate(far_first[1:], 1):
-                acc[i, o] = acc[i, o] + precv[i, p]
         return carry
 
-    lax.fori_loop(0, n_col + hops, step, 0)
+    lax.fori_loop(0, n_col + hops + 1, step, 0)
 
     for way in range(2):
         for j in range(n_step):

time: 111 us -> 102 us (0.919)
  the two profiles are of different devices: /device:TPU:22 before, /device:TPU:21 now
where the time goes in v3:
time: 102 us
  Pallas kernels  100 us (98%)
  local copies, waits for them, and re-layouts  1.67 us (2%)
    pallas_call x1, Pallas kernels, local_moe(): pl.pallas_call(functools.partial(moe_kernel, group, cap), out_shape=jax.S...  100 us

profile of v3, /device:TPU:21, one launch (start us, length us, event | category | flops | bytes accessed | tf_op | source)
XLA Modules:
  0.0 101.8 jit_solution(16738661913071857145)
XLA Ops:
  0.0 100.1 %shard_map.55 = bf16[64,2048]{1,0:T(8,128)(2,1)} custom-call(bf16[64,2048]{1,0:T(8,128)(2,1)} %x_hbm.1, s32[6,64]{1,0:T(8,128)} %bitcast.2, f32[6,64]{1,0:T(8,128)} %bitcast.3, bf16[4,2048,1408]{2,1,0:T(8,128)(2,1)} %up_hbm.1, bf16[4,1408,2048]{2,1,0:T(8,128)(2,1)} %down_hbm.1), custom_call_target="tpu_custom_call" | custom-call | tf_op jit(solution)/shard_map/pallas_call | solution.py:336
  100.1 1.7 %copy.7 = bf16[64,2048]{1,0:T(8,128)(2,1)} copy(bf16[64,2048]{1,0:T(8,128)(2,1)} %shard_map.55) | data formatting | bytes 524288

commit v4 on v3

--- a/solution.py
+++ b/solution.py
@@ -47,9 +47,9 @@
     def up_copy(e):
         return pltpu.make_async_copy(up_hbm.at[e], wup.at[e], up_sem.at[e])
 
-    def wd_copy(c):
-        slot = lax.rem(c, WD_SLOTS)
-        cols = pl.ds(pl.multiple_of(c * COLS, COLS), COLS)
+    def wd_copy(load):
+        slot = lax.rem(load, WD_SLOTS)
+        cols = pl.ds(pl.multiple_of(lax.rem(load, n_col) * COLS, COLS), COLS)
         return pltpu.make_async_copy(down_hbm.at[:, :, cols], wd.at[slot], wd_sem.at[slot])
 
     for e in range(n_exp):
@@ -207,12 +207,13 @@
     for o in range(n_chip):
         ob[o, pl.ds(slots, COLS - slots), :] = jnp.zeros((COLS - slots, COLS), bf16)
 
+    far_first = order[::-1]
+    n_last = n_chip - bounds[2]
+    pair_parts = ((0, 1), (1, n_last - 1), (n_last, n_chip - n_last))
+
     def pair_sum(c, k):
-        slot = lax.rem(c, 2)
-        part = pl.ds(k, 1 if k == 0 else n_chip - 1)
-        return remote(psend.at[slot, part], precv.at[c, part], ps_s.at[c, k], ps_r.at[c, k], partner)
-
-    far_first = order[::-1]
+        part = pl.ds(*pair_parts[k])
+        return remote(psend.at[lax.rem(c, 2), part], precv.at[c, part], ps_s.at[c, k], ps_r.at[c, k], partner)
 
     def half_sum(way, c):
         rows = pl.ds(way * half, half)
@@ -223,73 +224,107 @@
         return remote(acc.at[c, o], rfull.at[way, k - 1, c], f_s.at[way, k - 1, c], f_r.at[way, k - 1, c],
                       left if way else right)
 
-    def down_chunk(c):
-        slot = lax.rem(c, WD_SLOTS)
-        wd_copy(c).wait()
+    def down_chunk(c, last):
+        load = c if last else c + n_col
+        lo, hi = (bounds[2], n_chip) if last else (0, bounds[2])
+        slot = lax.rem(load, WD_SLOTS)
+        wd_copy(load).wait()
         for e in range(n_exp):
-            out = jnp.dot(hid[e], wd[slot, e], preferred_element_type=f32).astype(bf16)
-            for o in range(n_chip):
-                ob[o, pl.ds(e * chip_cap, chip_cap), :] = out[place[o] * chip_cap:(place[o] + 1) * chip_cap]
-
-        @pl.when(c + WD_SLOTS < n_col)
-        def _():
-            wd_copy(c + WD_SLOTS).start()
+            rows = hid[e, pl.ds(lo * chip_cap, (hi - lo) * chip_cap), :]
+            out = jnp.dot(rows, wd[slot, e], preferred_element_type=f32).astype(bf16)
+            for p in range(lo, hi):
+                ob[order[p], pl.ds(e * chip_cap, chip_cap), :] = out[(p - lo) * chip_cap:(p - lo + 1) * chip_cap]
+
+        @pl.when(load + WD_SLOTS < 2 * n_col)
+        def _():
+            wd_copy(load + WD_SLOTS).start()
 
         @pl.when(c >= 2)
         def _():
-            for k in range(2):
+            for k in (0, 1) if last else (2,):
                 pair_sum(c - 2, k).wait_send()
 
-        for p, o in enumerate(far_first):
+        for q in range(n_last) if last else range(n_last, n_chip):
+            o = far_first[q]
             got = jnp.dot(cmat[o], ob[o], preferred_element_type=f32)
             total = got[:LANES] + got[LANES:2 * LANES] + got[2 * LANES:]
             acc[c, o] = total[:tok]
-            psend[lax.rem(c, 2), p] = total[tok:]
-            if p == 0:
+            psend[lax.rem(c, 2), q] = total[tok:]
+            if q == 0:
                 pair_sum(c, 0).start()
-        pair_sum(c, 1).start()
-
-    def step(i, carry):
+        pair_sum(c, 1 if last else 2).start()
+
+    def stage(k, c):
+        if k == 0:
+            pair_sum(c, 0).wait_recv()
+            acc[c, hops] = acc[c, hops] + precv[c, 0]
+            for way in range(2):
+                half_sum(way, c).start()
+            return
+        if k < 3:
+            pair_sum(c, k).wait_recv()
+        if k == hops:
+            total = acc[c, 0] + precv[c, far_first.index(0)]
+            for way in range(2):
+                full_sum(way, hops - 1, c).wait_recv()
+                total = total + rfull[way, hops - 2, c]
+            cols = pl.ds(pl.multiple_of(c * COLS, COLS), COLS)
+            y_ref[:, cols] = total.astype(bf16)
+            return
+        for way in range(2):
+            o = hops + k if way == 0 else hops - k
+            acc[c, o] = acc[c, o] + precv[c, far_first.index(o)]
+            if k == 1:
+                half_sum(way, c).wait_recv()
+                rows = pl.ds(way * half, half)
+                acc[c, o, rows, :] = acc[c, o, rows, :] + rhalf[way, c]
+            else:
+                full_sum(way, k - 1, c).wait_recv()
+                acc[c, o] = acc[c, o] + rfull[way, k - 2, c]
+            full_sum(way, k, c).start()
+
+    lag = n_col - 2
+
+    def last_rows(i, carry):
         @pl.when(i < n_col)
         def _():
-            down_chunk(i)
-            pair_sum(i, 0).wait_recv()
-            acc[i, hops] = acc[i, hops] + precv[i, 0]
-            for way in range(2):
-                half_sum(way, i).start()
-            pair_sum(i, 1).wait_recv()
-            for p, o in enumerate(far_first[1:], 1):
-                acc[i, o] = acc[i, o] + precv[i, p]
-
-        for k in range(1, hops + 1):
-            c = i - k if k < hops else i - hops - 1
-
-            @pl.when(jnp.logical_and(c >= 0, c < n_col))
-            def _():
-                if k == 1:
-                    for way in range(2):
-                        half_sum(way, c).wait_recv()
-                        o = hops + 1 if way == 0 else hops - 1
-                        rows = pl.ds(way * half, half)
-                        acc[c, o, rows, :] = acc[c, o, rows, :] + rhalf[way, c]
-                        full_sum(way, 1, c).start()
-                elif k < hops:
-                    for way in range(2):
-                        full_sum(way, k - 1, c).wait_recv()
-                        o = hops + k if way == 0 else hops - k
-                        acc[c, o] = acc[c, o] + rfull[way, k - 2, c]
-                        full_sum(way, k, c).start()
-                else:
-                    total = acc[c, 0]
-                    for way in range(2):
-                        full_sum(way, hops - 1, c).wait_recv()
-                        total = total + rfull[way, hops - 2, c]
-                    cols = pl.ds(pl.multiple_of(c * COLS, COLS), COLS)
-                    y_ref[:, cols] = total.astype(bf16)
-
+            down_chunk(i, True)
+
+        @pl.when(i >= 1)
+        def _():
+            stage(0, i - 1)
+
+        @pl.when(i >= lag)
+        def _():
+            stage(1, i - lag)
         return carry
 
-    lax.fori_loop(0, n_col + hops + 1, step, 0)
+    early = n_col + 1 - lag
+    rest = n_col - early
+
+    def first_rows(i, carry):
+        down_chunk(i, False)
+
+        @pl.when(i < rest)
+        def _():
+            stage(1, i + early)
+
+        @pl.when(i >= rest)
+        def _():
+            stage(2, i - rest)
+        return carry
+
+    def finish(k, first):
+        def one(c, carry):
+            stage(k, c)
+            return carry
+        lax.fori_loop(first, n_col, one, 0)
+
+    lax.fori_loop(0, n_col + 1, last_rows, 0)
+    lax.fori_loop(0, n_col, first_rows, 0)
+    finish(2, early)
+    for k in range(3, hops + 1):
+        finish(k, 0)
 
     for way in range(2):
         for j in range(n_step):
@@ -309,7 +344,7 @@
 
         @pl.when(c >= n_col - 2)
         def _():
-            for k in range(2):
+            for k in range(3):
                 pair_sum(c, k).wait_send()
         return carry
 
@@ -355,7 +390,7 @@
                 dma, dma((n_exp,)), dma((WD_SLOTS,)),
                 dma((2, n_step)), dma((2, n_step)), dma((2, hops)), dma((2, hops)),
                 dma((n_chip, 2)), dma((n_chip, 2)), dma((n_chip,)), dma((n_chip,)),
-                dma((n_col, 2)), dma((n_col, 2)), dma((2, n_col)), dma((2, n_col)),
+                dma((n_col, 3)), dma((n_col, 3)), dma((2, n_col)), dma((2, n_col)),
                 dma((2, hops - 1, n_col)), dma((2, hops - 1, n_col)),
             ],
             compiler_params=pltpu.CompilerParams(

time: 102 us -> 99.3 us (0.974)
  Pallas kernels: 100 us -> 97.5 us
    pallas_call x1, Pallas kernels: 100 us -> 97.5 us  [local_moe(): pl.pallas_call(functools.partial(moe_kernel, group, cap), out_shape=jax.S...]
where the time goes in v4:
time: 99.3 us; the launch traced here: 99.2 us
  Pallas kernels  97.5 us (98%)
  local copies, waits for them, and re-layouts  1.67 us (2%)
    pallas_call x1, Pallas kernels, local_moe(): pl.pallas_call(functools.partial(moe_kernel, group, cap), out_shape=jax.S...  97.5 us

profile of v4, /device:TPU:21, one launch (start us, length us, event | category | flops | bytes accessed | tf_op | source)
XLA Modules:
  0.0 99.2 jit_solution(6320976768392993767)
XLA Ops:
  0.0 97.5 %shard_map.55 = bf16[64,2048]{1,0:T(8,128)(2,1)} custom-call(bf16[64,2048]{1,0:T(8,128)(2,1)} %x_hbm.1, s32[6,64]{1,0:T(8,128)} %bitcast.2, f32[6,64]{1,0:T(8,128)} %bitcast.3, bf16[4,2048,1408]{2,1,0:T(8,128)(2,1)} %up_hbm.1, bf16[4,1408,2048]{2,1,0:T(8,128)(2,1)} %down_hbm.1), custom_call_target="tpu_custom_call" | custom-call | tf_op jit(solution)/shard_map/pallas_call | solution.py:371
  97.5 1.7 %copy.7 = bf16[64,2048]{1,0:T(8,128)(2,1)} copy(bf16[64,2048]{1,0:T(8,128)(2,1)} %shard_map.55) | data formatting | bytes 524288

commit v5 on v4

--- a/solution.py
+++ b/solution.py
@@ -10,7 +10,9 @@
 MESH = pl.DeviceIdType.MESH
 COLS = 256
 LANES = 128
-WD_SLOTS = 3
+WD_SLOTS = 5
+PIECES = 4
+ROW_CUTS = 4
 
 
 def moe_kernel(group, cap, x_hbm, ids_ref, gate_ref, up_hbm, down_hbm, y_ref,
@@ -44,18 +46,22 @@
     metab[0, 0, pl.ds(0, top_k), pl.ds(0, tok)] = ids_ref[...].astype(f32)
     metab[0, 0, pl.ds(8, top_k), pl.ds(0, tok)] = gate_ref[...]
 
-    def up_copy(e):
-        return pltpu.make_async_copy(up_hbm.at[e], wup.at[e], up_sem.at[e])
-
-    def wd_copy(load):
+    def up_copies(e):
+        cut = d_model // ROW_CUTS
+        return [pltpu.make_async_copy(up_hbm.at[e, pl.ds(r * cut, cut)], wup.at[e, pl.ds(r * cut, cut)], up_sem.at[e, r])
+                for r in range(ROW_CUTS)]
+
+    def wd_copies(load):
         slot = lax.rem(load, WD_SLOTS)
         cols = pl.ds(pl.multiple_of(lax.rem(load, n_col) * COLS, COLS), COLS)
-        return pltpu.make_async_copy(down_hbm.at[:, :, cols], wd.at[slot], wd_sem.at[slot])
+        return [pltpu.make_async_copy(down_hbm.at[e, :, cols], wd.at[slot, e], wd_sem.at[slot, e]) for e in range(n_exp)]
 
     for e in range(n_exp):
-        up_copy(e).start()
-    for c in range(min(WD_SLOTS, n_col)):
-        wd_copy(jnp.int32(c)).start()
+        for copy in up_copies(e):
+            copy.start()
+    for c in range(WD_SLOTS):
+        for copy in wd_copies(jnp.int32(c)):
+            copy.start()
 
     barrier = pltpu.get_barrier_semaphore()
     for dev in (right, left, partner):
@@ -65,18 +71,19 @@
 
     steps = [[], []]
     for h in range(hops):
-        for b in range(2):
+        for b in range(PIECES):
             for way in range(2):
-                if h < hops - 1 or b == way:
+                if h < hops - 1 or b // (PIECES // 2) == way:
                     steps[way].append((h, b))
     n_step = len(steps[0])
+    piece = tok // PIECES
 
     def slot_of(way, h):
         return h if way == 0 else (n_chip - h) % n_chip
 
     def ring_x(way, j):
         h, b = steps[way][j]
-        rows = pl.ds(b * half, half)
+        rows = pl.ds(b * piece, piece)
         return remote(xb.at[slot_of(way, h), 0, rows], xb.at[slot_of(way, h + 1), 0, rows],
                       ag_s.at[way, j], ag_r.at[way, j], left if way else right)
 
@@ -85,7 +92,7 @@
                       mt_s.at[way, h], mt_r.at[way, h], left if way else right)
 
     def pair_x(o, b):
-        rows = pl.ds(b * half, half)
+        rows = pl.ds(b * piece, piece)
         return remote(xb.at[o, 0, rows], xb.at[o, 1, rows], pd_s.at[o, b], pd_r.at[o, b], partner)
 
     def pair_meta(o):
@@ -99,6 +106,7 @@
     order.append(hops)
     place = {o: p for p, o in enumerate(order)}
     bounds = [0, 3, 5, n_chip]
+    held = [p if p < bounds[2] else p - bounds[2] for p in range(n_chip)]
 
     tri_r = lax.broadcasted_iota(jnp.int32, (LANES, LANES), 0)
     tri_c = lax.broadcasted_iota(jnp.int32, (LANES, LANES), 1)
@@ -129,7 +137,7 @@
             rows_x = jnp.concatenate([xb[o, 0, :, cols], xb[o, 1, :, cols]], axis=0)
             got = jnp.dot(pick_all, rows_x, preferred_element_type=f32).astype(bf16)
             for e in range(n_exp):
-                xg[e, pl.ds(place[o] * chip_cap, chip_cap), cols] = got[e * chip_cap:(e + 1) * chip_cap]
+                xg[e, pl.ds(held[place[o]] * chip_cap, chip_cap), cols] = got[e * chip_cap:(e + 1) * chip_cap]
         weighted = [pick[e] * gate_rows[e] for e in range(n_exp)]
         weighted.append(jnp.zeros((COLS - slots, LANES), f32))
         rest = jnp.transpose(jnp.concatenate(weighted, axis=0))
@@ -140,16 +148,16 @@
 
     for way in range(2):
         ring_meta(way, 0).start()
-    for j in range(2):
+    for j in range(PIECES):
         for way in range(2):
             ring_x(way, j).start()
     pair_meta(0).start()
-    for b in range(2):
+    for b in range(PIECES):
         pair_x(0, b).start()
 
     def routed(o):
         pair_meta(o).wait_recv()
-        for b in range(2):
+        for b in range(PIECES):
             pair_x(o, b).wait_recv()
         route(o)
 
@@ -169,45 +177,37 @@
                 ring_x(way, steps[way].index(nxt)).start()
             pair_x(slot_of(way, h + 1), steps[way][j][1]).start()
 
-    def up_rows(phase, first, last):
-        rows = pl.ds(bounds[phase] * chip_cap, (bounds[phase + 1] - bounds[phase]) * chip_cap)
-
-        def expert(e, carry):
-            if phase == 0:
-                up_copy(e).wait()
-            for start in range(0, d_ff, COLS):
-                cols = pl.ds(start, min(COLS, d_ff - start))
-                raw = jnp.dot(xg[e, rows, :], wup[e, :, cols], preferred_element_type=f32)
-                hid[e, rows, cols] = jax.nn.gelu(raw, approximate=True).astype(bf16)
-            return carry
-
-        lax.fori_loop(first, last, expert, 0)
-
+    def up_rows(phase, e):
+        if phase == 0:
+            for copy in up_copies(e):
+                copy.wait()
+        lo, size = bounds[phase], (bounds[phase + 1] - bounds[phase]) * chip_cap
+        src, dst = pl.ds(held[lo] * chip_cap, size), pl.ds(lo * chip_cap, size)
+        for start in range(0, d_ff, COLS):
+            cols = pl.ds(start, min(COLS, d_ff - start))
+            raw = jnp.dot(xg[e, src, :], wup[e, :, cols], preferred_element_type=f32)
+            hid[e, dst, cols] = jax.nn.gelu(raw, approximate=True).astype(bf16)
+
+    far_first = order[::-1]
+    work = [lambda: (routed(1), routed(n_chip - 1))]
+    work += [functools.partial(up_rows, 0, e) for e in range(n_exp)]
+    work += [lambda: (routed(2), routed(n_chip - 2))]
+    work += [functools.partial(up_rows, 1, e) for e in range(n_exp)]
     routed(0)
-    gather_step(0)
-    gather_step(1)
-    routed(1)
-    routed(n_chip - 1)
-    gather_step(2)
-    up_rows(0, 0, n_exp // 2)
-    gather_step(3)
-    up_rows(0, n_exp // 2, n_exp)
-    routed(2)
-    routed(n_chip - 2)
-    gather_step(4)
-    up_rows(1, 0, n_exp // 2)
-    gather_step(5)
-    up_rows(1, n_exp // 2, n_exp)
-    routed(3)
-    routed(n_chip - 3)
-    gather_step(6)
-    routed(hops)
-    up_rows(2, 0, n_exp)
+    for j in range(n_step):
+        gather_step(j)
+        if j >= PIECES and work:
+            work.pop(0)()
+    for item in work:
+        item()
+    for p in range(bounds[2], n_chip):
+        routed(order[p])
+    for e in range(n_exp):
+        up_rows(2, e)
 
     for o in range(n_chip):
         ob[o, pl.ds(slots, COLS - slots), :] = jnp.zeros((COLS - slots, COLS), bf16)
 
-    far_first = order[::-1]
     n_last = n_chip - bounds[2]
     pair_parts = ((0, 1), (1, n_last - 1), (n_last, n_chip - n_last))
 
@@ -228,7 +228,8 @@
         load = c if last else c + n_col
         lo, hi = (bounds[2], n_chip) if last else (0, bounds[2])
         slot = lax.rem(load, WD_SLOTS)
-        wd_copy(load).wait()
+        for copy in wd_copies(load):
+            copy.wait()
         for e in range(n_exp):
             rows = hid[e, pl.ds(lo * chip_cap, (hi - lo) * chip_cap), :]
             out = jnp.dot(rows, wd[slot, e], preferred_element_type=f32).astype(bf16)
@@ -237,7 +238,8 @@
 
         @pl.when(load + WD_SLOTS < 2 * n_col)
         def _():
-            wd_copy(load + WD_SLOTS).start()
+            for copy in wd_copies(load + WD_SLOTS):
+                copy.start()
 
         @pl.when(c >= 2)
         def _():
@@ -333,7 +335,7 @@
             ring_meta(way, h).wait_send()
     for o in range(n_chip):
         pair_meta(o).wait_send()
-        for b in range(2):
+        for b in range(PIECES):
             pair_x(o, b).wait_send()
 
     def drain(c, carry):
@@ -367,7 +369,7 @@
         dma = pltpu.SemaphoreType.DMA
         any_spec = pl.BlockSpec(memory_space=pl.ANY)
         vmem_spec = pl.BlockSpec(memory_space=pltpu.VMEM)
-        n_step = 2 * hops - 1
+        n_step = PIECES * hops - PIECES // 2
         return pl.pallas_call(
             functools.partial(moe_kernel, group, cap),
             out_shape=jax.ShapeDtypeStruct((tok, d_model), bf16),
@@ -378,7 +380,7 @@
                 pltpu.VMEM((WD_SLOTS, n_exp, d_ff, COLS), bf16),
                 pltpu.VMEM((n_chip, 2, tok, d_model), bf16),
                 pltpu.VMEM((n_chip, 2, 16, LANES), f32),
-                pltpu.VMEM((n_exp, n_chip * 2 * cap, d_model), bf16),
+                pltpu.VMEM((n_exp, (n_chip - 3) * 2 * cap, d_model), bf16),
                 pltpu.VMEM((n_exp, n_chip * 2 * cap, d_ff), bf16),
                 pltpu.VMEM((n_chip, 3 * LANES, COLS), bf16),
                 pltpu.VMEM((n_chip, COLS, COLS), bf16),
@@ -387,9 +389,9 @@
                 pltpu.VMEM((n_col, n_chip, tok, COLS), f32),
                 pltpu.VMEM((2, n_col, tok // 2, COLS), f32),
                 pltpu.VMEM((2, hops - 1, n_col, tok, COLS), f32),
-                dma, dma((n_exp,)), dma((WD_SLOTS,)),
+                dma, dma((n_exp, ROW_CUTS)), dma((WD_SLOTS, n_exp)),
                 dma((2, n_step)), dma((2, n_step)), dma((2, hops)), dma((2, hops)),
-                dma((n_chip, 2)), dma((n_chip, 2)), dma((n_chip,)), dma((n_chip,)),
+                dma((n_chip, PIECES)), dma((n_chip, PIECES)), dma((n_chip,)), dma((n_chip,)),
                 dma((n_col, 3)), dma((n_col, 3)), dma((2, n_col)), dma((2, n_col)),
                 dma((2, hops - 1, n_col)), dma((2, hops - 1, n_col)),
             ],

time: 99.3 us -> 102 us (1.027)
  Pallas kernels: 97.5 us -> 100 us
    pallas_call x1, Pallas kernels: 97.5 us -> 100 us  [local_moe(): pl.pallas_call(functools.partial(moe_kernel, group, cap), out_shape=jax.S...]
where the time goes in v5:
time: 102 us
  Pallas kernels  100 us (98%)
  local copies, waits for them, and re-layouts  1.67 us (2%)
    pallas_call x1, Pallas kernels, local_moe(): pl.pallas_call(functools.partial(moe_kernel, group, cap), out_shape=jax.S...  100 us

profile of v5, /device:TPU:21, one launch (start us, length us, event | category | flops | bytes accessed | tf_op | source)
XLA Modules:
  0.0 102.2 jit_solution(10378842819176163622)
XLA Ops:
  0.0 100.5 %shard_map.55 = bf16[64,2048]{1,0:T(8,128)(2,1)} custom-call(bf16[64,2048]{1,0:T(8,128)(2,1)} %x_hbm.1, s32[6,64]{1,0:T(8,128)} %bitcast.2, f32[6,64]{1,0:T(8,128)} %bitcast.3, bf16[4,2048,1408]{2,1,0:T(8,128)(2,1)} %up_hbm.1, bf16[4,1408,2048]{2,1,0:T(8,128)(2,1)} %down_hbm.1), custom_call_target="tpu_custom_call" | custom-call | tf_op jit(solution)/shard_map/pallas_call | solution.py:373
  100.5 1.7 %copy.7 = bf16[64,2048]{1,0:T(8,128)(2,1)} copy(bf16[64,2048]{1,0:T(8,128)(2,1)} %shard_map.55) | data formatting | bytes 524288

commit v6 on v5

--- a/solution.py
+++ b/solution.py
@@ -12,7 +12,8 @@
 LANES = 128
 WD_SLOTS = 5
 PIECES = 4
-ROW_CUTS = 4
+ROW_CUTS = 1
+DOWN_CUTS = 1
 
 
 def moe_kernel(group, cap, x_hbm, ids_ref, gate_ref, up_hbm, down_hbm, y_ref,
@@ -54,13 +55,12 @@
     def wd_copies(load):
         slot = lax.rem(load, WD_SLOTS)
         cols = pl.ds(pl.multiple_of(lax.rem(load, n_col) * COLS, COLS), COLS)
-        return [pltpu.make_async_copy(down_hbm.at[e, :, cols], wd.at[slot, e], wd_sem.at[slot, e]) for e in range(n_exp)]
+        cut = n_exp // DOWN_CUTS
+        return [pltpu.make_async_copy(down_hbm.at[pl.ds(r * cut, cut), :, cols], wd.at[slot, pl.ds(r * cut, cut)], wd_sem.at[slot, r])
+                for r in range(DOWN_CUTS)]
 
     for e in range(n_exp):
         for copy in up_copies(e):
-            copy.start()
-    for c in range(WD_SLOTS):
-        for copy in wd_copies(jnp.int32(c)):
             copy.start()
 
     barrier = pltpu.get_barrier_semaphore()
@@ -177,6 +177,11 @@
                 ring_x(way, steps[way].index(nxt)).start()
             pair_x(slot_of(way, h + 1), steps[way][j][1]).start()
 
+    def start_down():
+        for c in range(WD_SLOTS):
+            for copy in wd_copies(jnp.int32(c)):
+                copy.start()
+
     def up_rows(phase, e):
         if phase == 0:
             for copy in up_copies(e):
@@ -189,19 +194,20 @@
             hid[e, dst, cols] = jax.nn.gelu(raw, approximate=True).astype(bf16)
 
     far_first = order[::-1]
-    work = [lambda: (routed(1), routed(n_chip - 1))]
-    work += [functools.partial(up_rows, 0, e) for e in range(n_exp)]
-    work += [lambda: (routed(2), routed(n_chip - 2))]
-    work += [functools.partial(up_rows, 1, e) for e in range(n_exp)]
+    first, second = [[functools.partial(up_rows, phase, e) for e in range(n_exp)] for phase in range(2)]
+
+    def routed_both(h):
+        routed(h)
+        routed(n_chip - h)
+
+    work = {4: [lambda: routed_both(1)], 5: first[:1], 6: first[1:3], 7: first[3:], 8: [start_down, lambda: routed_both(2), second[0]],
+            9: second[1:2], 10: second[2:3], 11: second[3:], 12: [lambda: routed_both(3)]}
     routed(0)
     for j in range(n_step):
         gather_step(j)
-        if j >= PIECES and work:
-            work.pop(0)()
-    for item in work:
-        item()
-    for p in range(bounds[2], n_chip):
-        routed(order[p])
+        for item in work.get(j, ()):
+            item()
+    routed(hops)
     for e in range(n_exp):
         up_rows(2, e)
 
@@ -389,7 +395,7 @@
                 pltpu.VMEM((n_col, n_chip, tok, COLS), f32),
                 pltpu.VMEM((2, n_col, tok // 2, COLS), f32),
                 pltpu.VMEM((2, hops - 1, n_col, tok, COLS), f32),
-                dma, dma((n_exp, ROW_CUTS)), dma((WD_SLOTS, n_exp)),
+                dma, dma((n_exp, ROW_CUTS)), dma((WD_SLOTS, DOWN_CUTS)),
                 dma((2, n_step)), dma((2, n_step)), dma((2, hops)), dma((2, hops)),
                 dma((n_chip, PIECES)), dma((n_chip, PIECES)), dma((n_chip,)), dma((n_chip,)),
                 dma((n_col, 3)), dma((n_col, 3)), dma((2, n_col)), dma((2, n_col)),

time: 102 us -> 98.2 us (0.963)
  Pallas kernels: 100 us -> 96.4 us
    pallas_call x1, Pallas kernels: 100 us -> 96.4 us  [local_moe(): pl.pallas_call(functools.partial(moe_kernel, group, cap), out_shape=jax.S...]
where the time goes in v6:
time: 98.2 us; the launch traced here: 98.1 us
  Pallas kernels  96.4 us (98%)
  local copies, waits for them, and re-layouts  1.67 us (2%)
    pallas_call x1, Pallas kernels, local_moe(): pl.pallas_call(functools.partial(moe_kernel, group, cap), out_shape=jax.S...  96.4 us

profile of v6, /device:TPU:21, one launch (start us, length us, event | category | flops | bytes accessed | tf_op | source)
XLA Modules:
  0.0 98.1 jit_solution(11521401990077748320)
XLA Ops:
  0.0 96.4 %shard_map.55 = bf16[64,2048]{1,0:T(8,128)(2,1)} custom-call(bf16[64,2048]{1,0:T(8,128)(2,1)} %x_hbm.1, s32[6,64]{1,0:T(8,128)} %bitcast.2, f32[6,64]{1,0:T(8,128)} %bitcast.3, bf16[4,2048,1408]{2,1,0:T(8,128)(2,1)} %up_hbm.1, bf16[4,1408,2048]{2,1,0:T(8,128)(2,1)} %down_hbm.1), custom_call_target="tpu_custom_call" | custom-call | tf_op jit(solution)/shard_map/pallas_call | solution.py:379
  96.4 1.7 %copy.7 = bf16[64,2048]{1,0:T(8,128)(2,1)} copy(bf16[64,2048]{1,0:T(8,128)(2,1)} %shard_map.55) | data formatting | bytes 524288

commit v7 on v6

--- a/solution.py
+++ b/solution.py
@@ -12,6 +12,7 @@
 LANES = 128
 WD_SLOTS = 5
 PIECES = 4
+UP_COLS = 768
 ROW_CUTS = 1
 DOWN_CUTS = 1
 
@@ -188,8 +189,8 @@
                 copy.wait()
         lo, size = bounds[phase], (bounds[phase + 1] - bounds[phase]) * chip_cap
         src, dst = pl.ds(held[lo] * chip_cap, size), pl.ds(lo * chip_cap, size)
-        for start in range(0, d_ff, COLS):
-            cols = pl.ds(start, min(COLS, d_ff - start))
+        for start in range(0, d_ff, UP_COLS):
+            cols = pl.ds(start, min(UP_COLS, d_ff - start))
             raw = jnp.dot(xg[e, src, :], wup[e, :, cols], preferred_element_type=f32)
             hid[e, dst, cols] = jax.nn.gelu(raw, approximate=True).astype(bf16)
 

time: 98.2 us -> 97 us (0.988)
  Pallas kernels: 96.4 us -> 95.2 us
    pallas_call x1, Pallas kernels: 96.4 us -> 95.2 us  [local_moe(): pl.pallas_call(functools.partial(moe_kernel, group, cap), out_shape=jax.S...]
where the time goes in v7:
time: 97 us; the launch traced here: 96.9 us
  Pallas kernels  95.2 us (98%)
  local copies, waits for them, and re-layouts  1.67 us (2%)
    pallas_call x1, Pallas kernels, local_moe(): pl.pallas_call(functools.partial(moe_kernel, group, cap), out_shape=jax.S...  95.2 us

profile of v7, /device:TPU:21, one launch (start us, length us, event | category | flops | bytes accessed | tf_op | source)
XLA Modules:
  0.0 96.9 jit_solution(9115930851628198019)
XLA Ops:
  0.0 95.2 %shard_map.55 = bf16[64,2048]{1,0:T(8,128)(2,1)} custom-call(bf16[64,2048]{1,0:T(8,128)(2,1)} %x_hbm.1, s32[6,64]{1,0:T(8,128)} %bitcast.2, f32[6,64]{1,0:T(8,128)} %bitcast.3, bf16[4,2048,1408]{2,1,0:T(8,128)(2,1)} %up_hbm.1, bf16[4,1408,2048]{2,1,0:T(8,128)(2,1)} %down_hbm.1), custom_call_target="tpu_custom_call" | custom-call | tf_op jit(solution)/shard_map/pallas_call | solution.py:380
  95.2 1.7 %copy.7 = bf16[64,2048]{1,0:T(8,128)(2,1)} copy(bf16[64,2048]{1,0:T(8,128)(2,1)} %shard_map.55) | data formatting | bytes 524288
